TPU v7x, 32 devices: a whole 2x2x4 slice. The times are simulated.
32 devices in a mesh: prow: 4 (over x, core), pcol: 8 (over z, y).
Axes of the slice: x: 2, y: 2, z: 4, core: 2. Of those that a mesh axis runs over, the one named last changes fastest.
Arguments:
- slab: float32 [16384, 2048], P('prow', 'pcol'), may hold values from -6 to 6
- panel: float32 [16384, 512], P(('prow', 'pcol')), may hold values from -0.25 to 0.25
- pivots: int32 [512], replicated, may hold values from 0 to 16383, as said below
- inv_lower: float32 [512, 512], replicated, as said below
- inv_upper: float32 [512, 512], replicated, as said below
Outputs:
- updated: float32 [16384, 2048], P('prow', 'pcol')
Inputs may be any that keep to these rules, and one draw needn't show every extreme that they name: `pivots`: 512 distinct row indices. `inv_lower`: unit lower triangular. `inv_upper`: upper triangular with a positive diagonal.
All inputs are finite; a program needn't handle non-finite values.
Results may differ from a plain program's by a relative error of at most 0.000061.
Values sent between devices are 32-bit elements; how exact they have to be, the bound alone decides.
A program may use at most 64 MiB of HBM per device.

v0:
```python
import jax
import jax.numpy as jnp
from jax import lax
from jax.sharding import PartitionSpec as P


def local(slab, panel, pivots, inv_lower, inv_upper):
    row_count = slab.shape[0]
    first_row = lax.axis_index("prow") * row_count
    local_index = pivots - first_row
    inside = (local_index >= 0) & (local_index < row_count)
    safe_index = jnp.where(inside, local_index, 0)
    picked = jnp.where(inside[:, None], jnp.take(slab, safe_index, axis=0), 0.0)
    pivot_rows = lax.psum(picked, "prow")
    upper_block = jnp.dot(
        inv_lower, pivot_rows, precision=lax.Precision.HIGHEST, preferred_element_type=jnp.float32
    )
    own_lower = jnp.dot(
        panel, inv_upper, precision=lax.Precision.HIGHEST, preferred_element_type=jnp.float32
    )
    product = jnp.dot(
        lax.all_gather(own_lower, "pcol", axis=0, tiled=True),
        upper_block,
        precision=lax.Precision.HIGHEST,
        preferred_element_type=jnp.float32,
    )
    updated = slab - product
    target = jnp.where(inside, local_index, row_count)
    return updated.at[target].set(upper_block, mode="drop")


def solution(mesh):
    return jax.shard_map(
        local,
        mesh=mesh,
        in_specs=(P("prow", "pcol"), P(("prow", "pcol"), None), P(), P(), P()),
        out_specs=P("prow", "pcol"),
        check_vma=False,
    )
```

profile of v0, /device:TPU:0, one launch (start us, length us, event | category | flops | bytes accessed | tf_op | source)
XLA Modules:
  0.0 168.0 jit_solution(13603019011698801581)
XLA Ops:
  7.4 0.0 copy-start
  7.4 0.0 copy-start.1
  7.4 0.0 all-reduce.2.cloned.1.call-start
  7.4 0.8 compare_and_fusion
  8.2 0.0 copy-start.3
  8.2 3.8 %gather_fusion = f32[512,256]{1,0:T(8,128)S(1)} fusion(f32[4096,256]{1,0:T(8,128)} %param.5, s32[1024]{0:T(1024)S(1)} %pad_clamp_fusion), kind=kCustom, calls=%fused_computation | custom fusion | bytes 1050624 | tf_op jit(solution)/shard_map/jit(_take)/gather | solution.py:13
  12.0 1.0 select_select_fusion
  13.0 0.0 copy-start.2
  13.0 0.0 all-reduce.2.cloned.1.call-update
  13.1 0.0 all-gather.2.cloned.1.call-start
  13.1 0.0 copy-done
  13.1 0.0 copy-done.1
  13.1 2.8 %fusion = f32[512,512]{1,0:T(8,128)} fusion(f32[512,512]{1,0:T(8,128)S(1)} %copy-done, f32[512,512]{1,0:T(8,128)S(1)} %copy-done.1), kind=kOutput, calls=%fused_computation.9 | convolution fusion | flops 1610612736 | bytes 3145728 | tf_op jit(solution)/shard_map/dot_general | solution.py:18
  16.0 0.0 all-gather.2.cloned.1.call-update
  16.0 0.0 copy-done.3
  16.0 33.5 %all-reduce.2.cloned.1.call-done = f32[512,256]{1,0:T(8,128)} async-done(((f32[512,256]{1,0:T(8,128)}), f32[512,256]{1,0:T(8,128)}) %all-reduce.2.cloned.1.call-update) | async-done | bytes 524304 | tf_op jit(solution)/shard_map/psum | solution.py:14
  49.5 0.0 copy-done.2
  49.5 2.9 %fusion.1 = f32[256,512]{1,0:T(8,128)S(1)} fusion(f32[512,256]{1,0:T(8,128)} %all-reduce.2.cloned.1.call-done, f32[512,512]{1,0:T(8,128)S(1)} %copy-done.2), kind=kOutput, calls=%fused_computation.10 | convolution fusion | flops 805306368 | bytes 2097152 | tf_op jit(solution)/shard_map/dot_general | solution.py:15
  52.4 0.2 copy.6
  52.6 90.4 %all-gather.2.cloned.1.call-done = f32[4096,512]{1,0:T(8,128)} async-done(((f32[512,512]{1,0:T(8,128)}), f32[4096,512]{1,0:T(8,128)}) %all-gather.2.cloned.1.call-update) | async-done | bytes 8388624 | tf_op jit(solution)/shard_map/all_gather | solution.py:22
  143.0 11.2 %convolution_subtract_fusion = f32[4096,256]{1,0:T(8,128)} fusion(f32[4096,256]{1,0:T(8,128)} %param.5, f32[4096,512]{1,0:T(8,128)} %all-gather.2.cloned.1.call-done, f32[256,512]{1,0:T(8,128)S(1)} %fusion.1), kind=kOutput, calls=%fused_computation.2 | convolution fusion | flops 6443499520 | bytes 17301504 | tf_op jit(solution)/shard_map/dot_general | solution.py:21
  154.2 6.4 %scatter_fusion = f32[4096,256]{1,0:T(8,128)} fusion(f32[4096,256]{1,0:T(8,128)} %convolution_subtract_fusion, s32[512]{0:T(512)S(1)} %compare_select_fusion, f32[512,256]{1,0:T(8,128)S(1)} %copy.6), kind=kCustom, calls=%fused_computation.1 | custom fusion | bytes 1574912 | tf_op jit(solution)/shard_map/scatter | solution.py:29
  (2 shorter events, 0.0 us)
Async XLA Ops:
  7.4 5.8 %copy-start = (f32[512,512]{1,0:T(8,128)S(1)}, f32[512,512]{1,0:T(8,128)}, u32[]{:S(2)}) copy-start(f32[512,512]{1,0:T(8,128)} %param.6) | copy-start | bytes 3145732
  7.4 5.8 %copy-start.1 = (f32[512,512]{1,0:T(8,128)S(1)}, f32[512,512]{1,0:T(8,128)}, u32[]{:S(2)}) copy-start(f32[512,512]{1,0:T(8,128)} %param.9) | copy-start | bytes 3145732
  7.4 42.1 %all-reduce.2.cloned.1.call-start = ((), (), s32[]{:S(2)}) async-start(), calls=%async_computation.1 | async-start | bytes 1048576 | tf_op jit(solution)/shard_map/psum | solution.py:14
  8.2 7.8 %copy-start.3 = (s32[512]{0:T(512)S(1)}, s32[512]{0:T(512)}, u32[]{:S(2)}) copy-start(s32[512]{0:T(512)} %param.7) | copy-start | bytes 6148
  13.0 36.4 %copy-start.2 = (f32[512,512]{1,0:T(8,128)S(1)}, f32[512,512]{1,0:T(8,128)}, u32[]{:S(2)}) copy-start(f32[512,512]{1,0:T(8,128)} %param.8) | copy-start | bytes 3145732
  13.1 129.9 %all-gather.2.cloned.1.call-start = ((), (), s32[]{:S(2)}) async-start(), calls=%async_computation | async-start | bytes 9437184 | tf_op jit(solution)/shard_map/all_gather | solution.py:22
Sparse Core Ops, SparseCore 0:
  13.2 36.2 all-reduce.1
Sparse Core Ops, SparseCore 1:
  16.1 126.9 all-gather.1
where the time goes:
time: 168 us
  waiting for transfers between devices  124 us (74%)
  matrix products  16.9 us (10%)
  between operations  14.9 us (9%)
  local copies, waits for them, and re-layouts  10.4 us (6%)
  other arithmetic  1.89 us (1%)
    all_gather x1, waiting for transfers between devices, local(): lax.all_gather(own_lower, 'pcol', axis=0, tiled=True)  90.4 us
    psum x1, waiting for transfers between devices, local(): pivot_rows = lax.psum(picked, 'prow')  33.5 us
    dot_general x1, matrix products, local(): jnp.dot(lax.all_gather(own_lower, 'pcol', axis=0, tiled=True), upper_bloc...  11.2 us
    scatter x1, local copies, waits for them, and re-layouts, local(): return updated.at[target].set(upper_block, mode='drop')  6.39 us
    gather x1, local copies, waits for them, and re-layouts, local(): picked = jnp.where(inside[:, None], jnp.take(slab, safe_index, axis=0), 0.0)  3.76 us
  transfers between devices with their start and end apart: 2, of which 2 were waited for; matrix products, arithmetic and copies ran while one was open for 4% of the time, Pallas kernels for 0%

commit v1 on v0

v1 whole, which is shorter than its diff:
```python
import functools

import jax
import jax.numpy as jnp
from jax import lax
from jax.experimental import pallas as pl
from jax.experimental.pallas import tpu as pltpu
from jax.sharding import PartitionSpec as P

MESH = pl.DeviceIdType.MESH
HIGHEST = lax.Precision.HIGHEST
F32 = jnp.float32


def dot(a, b):
    return jnp.dot(a, b, precision=HIGHEST, preferred_element_type=F32)


def kernel(
    n_x, n_z, parts,
    slab_ref, panel_ref, pivots_ref, pivot_row_ref, inv_lower_ref, inv_upper_ref,
    out_ref,
    slab, raw, lower, stage, landed, inv_lower, inv_upper,
    picked, partner_part, chip_sum, from_x, total, halves, upper, upper_peer,
    load_sem, link_send, link_recv, product_send, product_recv, out_sem,
    pick_send, pick_recv, x_send, x_recv, half_send, half_recv,
):
    prow = lax.axis_index("prow")
    pcol = lax.axis_index("pcol")
    x, core = prow // 2, prow % 2
    z, y = pcol // 2, pcol % 2
    rows = panel_ref.shape[0]
    nb = panel_ref.shape[1]
    piece = rows // parts
    row_count, columns = slab_ref.shape
    half = columns // 2
    first_row = prow * row_count
    partner = {"prow": x * 2 + 1 - core}
    peer = {"pcol": z * 2 + 1 - y}
    left = {"pcol": (z - 1) * 2 + y}
    right = {"pcol": (z + 1) * 2 + y}
    has_left, has_right = z > 0, z < n_z - 1

    loads = [
        pltpu.make_async_copy(slab_ref, slab, load_sem.at[0]),
        pltpu.make_async_copy(panel_ref, raw.at[z], load_sem.at[1]),
        pltpu.make_async_copy(inv_upper_ref, inv_upper, load_sem.at[2]),
        pltpu.make_async_copy(inv_lower_ref, inv_lower, load_sem.at[3]),
    ]
    for load in loads:
        load.start()

    barrier = pltpu.get_barrier_semaphore()
    fixed = [partner, peer] + [
        {"prow": lax.rem(x + o, n_x) * 2 + core} for o in range(1, n_x)
    ]
    for device in fixed:
        pl.semaphore_signal(barrier, inc=1, device_id=device, device_id_type=MESH)
    for exists, device in ((has_left, left), (has_right, right)):
        @pl.when(exists)
        def _():
            pl.semaphore_signal(barrier, inc=1, device_id=device, device_id_type=MESH)
    n_peers = len(fixed) + has_left.astype(jnp.int32) + has_right.astype(jnp.int32)
    pl.semaphore_wait(barrier, n_peers)

    def slot(direction, step, g):
        return (direction * (n_z - 1) + step) * parts + g

    def send(direction, step, g):
        block = z - step if direction == 0 else z + step
        span = pl.ds(g * piece, piece)
        source = panel_ref.at[span] if isinstance(step, int) else raw.at[block, span]
        return pltpu.make_async_remote_copy(
            src_ref=source,
            dst_ref=raw.at[block, span],
            send_sem=link_send.at[slot(direction, step, g)],
            recv_sem=link_recv.at[slot(direction, step, g)],
            device_id=right if direction == 0 else left,
            device_id_type=MESH,
        )

    def sends(direction, step):
        if direction == 0:
            return has_right & (z - step >= 0)
        return has_left & (z + step < n_z)

    def receives(direction, step):
        if direction == 0:
            return z - 1 - step >= 0
        return z + 1 + step < n_z

    def arrived(direction, step, g):
        block = z - 1 - step if direction == 0 else z + 1 + step
        span = pl.ds(g * piece, piece)
        pltpu.make_async_remote_copy(
            src_ref=raw.at[block, span],
            dst_ref=raw.at[block, span],
            send_sem=link_send.at[slot(direction, step, g)],
            recv_sem=link_recv.at[slot(direction, step, g)],
            device_id=left if direction == 0 else right,
            device_id_type=MESH,
        ).wait_recv()
        return block

    for g in range(parts):
        for direction in (0, 1):
            @pl.when(sends(direction, 0))
            def _():
                send(direction, 0, g).start()

    loads[0].wait()

    def pick(k, carry):
        local = pivots_ref[k] - first_row
        inside = (local >= 0) & (local < row_count)
        row = slab[pl.ds(jnp.where(inside, local, 0), 1), :]
        row = jnp.where(inside, row, 0.0)
        picked[0, pl.ds(k, 1), :] = row[:, :half]
        picked[1, pl.ds(k, 1), :] = row[:, half:]
        return carry

    lax.fori_loop(0, nb, pick, 0, unroll=8)

    def remote(source, target, send_sem, recv_sem, device):
        return pltpu.make_async_remote_copy(
            src_ref=source, dst_ref=target, send_sem=send_sem, recv_sem=recv_sem,
            device_id=device, device_id_type=MESH,
        )

    pick_copy = remote(picked.at[1 - core], partner_part, pick_send, pick_recv, partner)
    pick_copy.start()

    def pivot_hits(block, side, g):
        row = first_row + (block * 2 + side) * rows + g * piece
        ids = row + lax.broadcasted_iota(jnp.int32, (piece, nb), 0)
        hits = jnp.where(ids == pivot_row_ref[...], 1.0, 0.0)
        return hits, jnp.max(hits, axis=1, keepdims=True) > 0.0

    def make_lower(block, g):
        span = pl.ds(g * piece, piece)
        solved = dot(raw[block, span, :], inv_upper[...])
        hits, is_pivot = pivot_hits(block, y, g)
        lower[block, span, :] = jnp.where(is_pivot, -hits, solved)

    pick_copy.wait()
    chip_sum[...] = picked[core] + partner_part[...]
    x_copies = []
    for o in range(1, n_x):
        device = {"prow": lax.rem(x + o, n_x) * 2 + core}
        copy = remote(chip_sum, from_x.at[o - 1], x_send.at[o - 1], x_recv.at[o - 1], device)
        copy.start()
        x_copies.append(copy)

    loads[1].wait()
    loads[2].wait()
    loads[3].wait()
    lax.fori_loop(0, parts, lambda g, c: (make_lower(z, g), c)[1], 0)

    for copy in x_copies:
        copy.wait()
    summed = chip_sum[...]
    for o in range(1, n_x):
        summed = summed + from_x[o - 1]
    total[...] = summed
    halves[core] = dot(inv_lower[...], total[...])
    to_peer = remote(
        halves.at[core], halves.at[2 + core], half_send.at[0], half_recv.at[0], peer
    )
    to_partner = remote(
        halves.at[core], halves.at[core], half_send.at[1], half_recv.at[1], partner
    )
    to_peer.start()
    to_partner.start()

    def pass_on(step, g):
        for direction in (0, 1):
            @pl.when(receives(direction, step))
            def _():
                arrived(direction, step, g)

            @pl.when(receives(direction, step) & sends(direction, step + 1))
            def _():
                send(direction, step + 1, g).start()

    def blocks_of(stage_index):
        step = stage_index - 1
        return (
            (receives(0, step), z - 1 - step),
            (receives(1, step), z + 1 + step),
        )

    def first_stage(g, carry):
        pass_on(jnp.int32(0), g)
        for exists, block in blocks_of(1):
            @pl.when(exists)
            def _():
                make_lower(block, g)
        return carry

    lax.fori_loop(0, parts, first_stage, 0)

    to_partner.wait()
    to_peer.wait()
    onward = remote(
        halves.at[2 + core], halves.at[2 + core], half_send.at[2], half_recv.at[2], partner
    )
    onward.start()
    upper[:, :half] = halves[0]
    upper[:, half:] = halves[1]
    onward.wait()
    upper_peer[:, :half] = halves[2]
    upper_peer[:, half:] = halves[3]

    def product_copy(block, g):
        span = pl.ds(g * piece, piece)
        index = block * parts + g
        return remote(
            stage.at[block, span], landed.at[block, span],
            product_send.at[index], product_recv.at[index], peer,
        )

    def out_copy(block, side, g):
        start = (block * 2 + side) * rows + g * piece
        span = pl.ds(pl.multiple_of(start, 8), piece)
        index = (block * 2 + side) * parts + g
        return pltpu.make_async_copy(slab.at[span], out_ref.at[span], out_sem.at[index])

    def finish(block, side, g, product, is_pivot):
        start = (block * 2 + side) * rows + g * piece
        span = pl.ds(pl.multiple_of(start, 8), piece)
        slab[span, :] = jnp.where(is_pivot, 0.0, slab[span, :]) - product
        out_copy(block, side, g).start()

    def multiply(block, g):
        span = pl.ds(g * piece, piece)
        stage[block, span, :] = dot(lower[block, span, :], upper_peer[...])
        product_copy(block, g).start()
        _, is_pivot = pivot_hits(block, y, g)
        finish(block, y, g, dot(lower[block, span, :], upper[...]), is_pivot)

    def take(block, g):
        product_copy(block, g).wait_recv()
        _, is_pivot = pivot_hits(block, 1 - y, g)
        span = pl.ds(g * piece, piece)
        finish(block, 1 - y, g, landed[block, span, :], is_pivot)

    lax.fori_loop(0, parts, lambda g, c: (multiply(z, g), c)[1], 0)

    def second_stage(g, carry):
        for exists, block in blocks_of(1):
            @pl.when(exists)
            def _():
                multiply(block, g)
        return carry

    lax.fori_loop(0, parts, second_stage, 0)

    def late_stage(i, carry):
        stage_index, g = 2 + i // parts, i % parts
        pass_on(stage_index - 1, g)
        for exists, block in blocks_of(stage_index):
            @pl.when(exists)
            def _():
                make_lower(block, g)
                multiply(block, g)

        @pl.when(stage_index == 2)
        def _():
            take(z, g)

        for exists, block in blocks_of(stage_index - 2):
            @pl.when(exists & (stage_index > 2))
            def _():
                take(block, g)
        return carry

    lax.fori_loop(0, (n_z - 2) * parts, late_stage, 0)

    def last_stage(i, carry):
        stage_index, g = n_z - 2 + i // parts, i % parts

        if n_z == 2:
            @pl.when(stage_index == 0)
            def _():
                take(z, g)

        for exists, block in blocks_of(stage_index):
            @pl.when(exists & (stage_index > 0))
            def _():
                take(block, g)
        return carry

    lax.fori_loop(0, 2 * parts, last_stage, 0)

    def settle(i, carry):
        block, g = i // parts, i % parts
        product_copy(block, g).wait_send()
        out_copy(block, 0, g).wait()
        out_copy(block, 1, g).wait()
        return carry

    lax.fori_loop(0, n_z * parts, settle, 0)

    def settle_links(i, carry):
        step, g = i // parts, i % parts
        for direction in (0, 1):
            @pl.when(sends(direction, step))
            def _():
                send(direction, step, g).wait_send()
        return carry

    lax.fori_loop(0, (n_z - 1) * parts, settle_links, 0)


def solution(mesh):
    n_prow, n_pcol = mesh.shape["prow"], mesh.shape["pcol"]
    n_x, n_z, parts = n_prow // 2, n_pcol // 2, 4

    def local(slab, panel, pivots, inv_lower, inv_upper):
        (row_count, columns), (rows, nb) = slab.shape, panel.shape
        half = columns // 2
        links = 2 * (n_z - 1) * parts
        any_space = pl.BlockSpec(memory_space=pl.ANY)
        dma = pltpu.SemaphoreType.DMA
        flops = 2 * row_count * nb * (nb + columns)
        return pl.pallas_call(
            functools.partial(kernel, n_x, n_z, parts),
            out_shape=jax.ShapeDtypeStruct(slab.shape, slab.dtype),
            in_specs=[
                any_space,
                any_space,
                pl.BlockSpec(memory_space=pltpu.SMEM),
                pl.BlockSpec(memory_space=pltpu.VMEM),
                any_space,
                any_space,
            ],
            out_specs=any_space,
            scratch_shapes=[
                pltpu.VMEM((row_count, columns), F32),
                pltpu.VMEM((n_z, rows, nb), F32),
                pltpu.VMEM((n_z, rows, nb), F32),
                pltpu.VMEM((n_z, rows, columns), F32),
                pltpu.VMEM((n_z, rows, columns), F32),
                pltpu.VMEM((nb, nb), F32),
                pltpu.VMEM((nb, nb), F32),
                pltpu.VMEM((2, nb, half), F32),
                pltpu.VMEM((nb, half), F32),
                pltpu.VMEM((nb, half), F32),
                pltpu.VMEM((max(n_x - 1, 1), nb, half), F32),
                pltpu.VMEM((nb, half), F32),
                pltpu.VMEM((4, nb, half), F32),
                pltpu.VMEM((nb, columns), F32),
                pltpu.VMEM((nb, columns), F32),
                dma((4,)),
                dma((links,)),
                dma((links,)),
                dma((n_z * parts,)),
                dma((n_z * parts,)),
                dma((2 * n_z * parts,)),
                dma,
                dma,
                dma((max(n_x - 1, 1),)),
                dma((max(n_x - 1, 1),)),
                dma((3,)),
                dma((3,)),
            ],
            compiler_params=pltpu.CompilerParams(
                collective_id=0, has_side_effects=True, vmem_limit_bytes=60 * 2**20
            ),
            cost_estimate=pl.CostEstimate(
                flops=flops, bytes_accessed=8 * slab.size, transcendentals=0
            ),
        )(slab, panel, pivots, pivots.reshape(1, nb), inv_lower, inv_upper)

    return jax.shard_map(
        local,
        mesh=mesh,
        in_specs=(P("prow", "pcol"), P(("prow", "pcol"), None), P(), P(), P()),
        out_specs=P("prow", "pcol"),
        check_vma=False,
    )
```

time: 168 us -> 86.3 us (0.51)
  waiting for transfers between devices: 124 us -> 0 us
  Pallas kernels: 0 us -> 81.7 us
  matrix products: 16.9 us -> 0 us
  between operations: 14.9 us -> 0.01 us
  local copies, waits for them, and re-layouts: 10.4 us -> 4.47 us
  other arithmetic: 1.89 us -> 0 us
    all_gather x1 -> x0, waiting for transfers between devices: 90.4 us -> none  [local(): lax.all_gather(own_lower, 'pcol', axis=0, tiled=True)]
    pallas_call x0 -> x1, Pallas kernels: none -> 81.7 us  [local(): pl.pallas_call(functools.partial(kernel, n_x, n_z, parts), out_shape=jax....]
    psum x1 -> x0, waiting for transfers between devices: 33.5 us -> none  [local(): pivot_rows = lax.psum(picked, 'prow')]
    dot_general x3 -> x0, matrix products: 16.9 us -> none  [the longest x1 11.2 us: local(): jnp.dot(lax.all_gather(own_lower, 'pcol', axis=0, tiled=True), upper_bloc...]
    scatter x1 -> x0, local copies, waits for them, and re-layouts: 6.39 us -> none  [local(): return updated.at[target].set(upper_block, mode='drop')]
    unnamed x8 -> x1, local copies, waits for them, and re-layouts: 0.02 us -> 4.47 us
    gather x1 -> x0, local copies, waits for them, and re-layouts: 3.76 us -> none  [local(): picked = jnp.where(inside[:, None], jnp.take(slab, safe_index, axis=0), 0.0)]
  transfers between devices with their start and end apart: 2 -> 0, of which waited for: 2 -> 0; matrix products, arithmetic and copies ran while one was open for 4% -> 0% of each run, Pallas kernels for 0% -> 0%
where the time goes in v1:
time: 86.3 us; the launch traced here: 86.1 us
  Pallas kernels  81.7 us (95%)
  local copies, waits for them, and re-layouts  4.47 us (5%)
    pallas_call x1, Pallas kernels, local(): pl.pallas_call(functools.partial(kernel, n_x, n_z, parts), out_shape=jax....  81.7 us
    unnamed x1, local copies, waits for them, and re-layouts  4.47 us

profile of v1, /device:TPU:0, one launch (start us, length us, event | category | flops | bytes accessed | tf_op | source)
XLA Modules:
  0.0 86.1 jit_solution(17325547964984877070)
XLA Ops:
  0.0 81.7 %shard_map.55 = f32[4096,256]{1,0:T(8,128)} custom-call(f32[4096,256]{1,0:T(8,128)} %slab_ref.1, f32[512,512]{1,0:T(8,128)} %panel_ref.1, s32[512]{0:T(512)} %pivots_ref.1, s32[1,512]{1,0:T(1,128)} %bitcast.1, f32[512,512]{1,0:T(8,128)} %inv_lower_ref.1, f32[512,512]{1,0:T(8,128)} %inv_upper_ref.1), custom_call_target="tpu_custom_call" | custom-call | flops 3221225472 | bytes 8388608 | tf_op jit(solution)/shard_map/pallas_call | solution.py:326
  81.7 4.5 %copy.7 = f32[4096,256]{1,0:T(8,128)} copy(f32[4096,256]{1,0:T(8,128)} %shard_map.55) | data formatting | bytes 8388608

commit v2 on v1

--- a/solution.py
+++ b/solution.py
@@ -10,21 +10,37 @@
 MESH = pl.DeviceIdType.MESH
 HIGHEST = lax.Precision.HIGHEST
 F32 = jnp.float32
+BF16 = jnp.bfloat16
 
 
 def dot(a, b):
     return jnp.dot(a, b, precision=HIGHEST, preferred_element_type=F32)
+
+
+def split(a):
+    high = a.astype(BF16)
+    return high, (a - high.astype(F32)).astype(BF16)
+
+
+def dot_split(a_high, a_low, b_high, b_low):
+    rows = a_high.shape[0]
+    both = jnp.dot(
+        jnp.concatenate([a_high, a_low], axis=0), b_high, preferred_element_type=F32
+    )
+    cross = jnp.dot(a_high, b_low, preferred_element_type=F32)
+    return both[:rows] + (both[rows:] + cross)
 
 
 def kernel(
     n_x, n_z, parts,
     slab_ref, panel_ref, pivots_ref, pivot_row_ref, inv_lower_ref, inv_upper_ref,
     out_ref,
-    slab, raw, lower, stage, landed, inv_lower, inv_upper,
-    picked, partner_part, chip_sum, from_x, total, halves, upper, upper_peer,
-    load_sem, link_send, link_recv, product_send, product_recv, out_sem,
+    raw, lower, stage, landed, inv_lower, inv_upper, inv_split,
+    picked, partner_part, chip_sum, from_x, total, halves, upper,
+    load_sem, link_send, link_recv, product_send, product_recv,
     pick_send, pick_recv, x_send, x_recv, half_send, half_recv,
 ):
+    slab = out_ref
     prow = lax.axis_index("prow")
     pcol = lax.axis_index("pcol")
     x, core = prow // 2, prow % 2
@@ -138,9 +154,12 @@
 
     def make_lower(block, g):
         span = pl.ds(g * piece, piece)
-        solved = dot(raw[block, span, :], inv_upper[...])
+        high, low = split(raw[block, span, :])
+        solved = dot_split(high, low, inv_split[0], inv_split[1])
         hits, is_pivot = pivot_hits(block, y, g)
-        lower[block, span, :] = jnp.where(is_pivot, -hits, solved)
+        high, low = split(jnp.where(is_pivot, -hits, solved))
+        lower[0, block, span, :] = high
+        lower[1, block, span, :] = low
 
     pick_copy.wait()
     chip_sum[...] = picked[core] + partner_part[...]
@@ -154,6 +173,7 @@
     loads[1].wait()
     loads[2].wait()
     loads[3].wait()
+    inv_split[0], inv_split[1] = split(inv_upper[...])
     lax.fori_loop(0, parts, lambda g, c: (make_lower(z, g), c)[1], 0)
 
     for copy in x_copies:
@@ -205,11 +225,15 @@
         halves.at[2 + core], halves.at[2 + core], half_send.at[2], half_recv.at[2], partner
     )
     onward.start()
-    upper[:, :half] = halves[0]
-    upper[:, half:] = halves[1]
+    for i in (0, 1):
+        upper[0, :, i * half:(i + 1) * half], upper[1, :, i * half:(i + 1) * half] = (
+            split(halves[i])
+        )
     onward.wait()
-    upper_peer[:, :half] = halves[2]
-    upper_peer[:, half:] = halves[3]
+    for i in (2, 3):
+        upper[0, :, i * half:(i + 1) * half], upper[1, :, i * half:(i + 1) * half] = (
+            split(halves[i])
+        )
 
     def product_copy(block, g):
         span = pl.ds(g * piece, piece)
@@ -219,24 +243,20 @@
             product_send.at[index], product_recv.at[index], peer,
         )
 
-    def out_copy(block, side, g):
-        start = (block * 2 + side) * rows + g * piece
-        span = pl.ds(pl.multiple_of(start, 8), piece)
-        index = (block * 2 + side) * parts + g
-        return pltpu.make_async_copy(slab.at[span], out_ref.at[span], out_sem.at[index])
-
     def finish(block, side, g, product, is_pivot):
         start = (block * 2 + side) * rows + g * piece
         span = pl.ds(pl.multiple_of(start, 8), piece)
         slab[span, :] = jnp.where(is_pivot, 0.0, slab[span, :]) - product
-        out_copy(block, side, g).start()
 
     def multiply(block, g):
         span = pl.ds(g * piece, piece)
-        stage[block, span, :] = dot(lower[block, span, :], upper_peer[...])
+        products = dot_split(
+            lower[0, block, span, :], lower[1, block, span, :], upper[0], upper[1]
+        )
+        stage[block, span, :] = products[:, columns:]
         product_copy(block, g).start()
         _, is_pivot = pivot_hits(block, y, g)
-        finish(block, y, g, dot(lower[block, span, :], upper[...]), is_pivot)
+        finish(block, y, g, products[:, :columns], is_pivot)
 
     def take(block, g):
         product_copy(block, g).wait_recv()
@@ -295,8 +315,6 @@
     def settle(i, carry):
         block, g = i // parts, i % parts
         product_copy(block, g).wait_send()
-        out_copy(block, 0, g).wait()
-        out_copy(block, 1, g).wait()
         return carry
 
     lax.fori_loop(0, n_z * parts, settle, 0)
@@ -320,43 +338,41 @@
         (row_count, columns), (rows, nb) = slab.shape, panel.shape
         half = columns // 2
         links = 2 * (n_z - 1) * parts
-        any_space = pl.BlockSpec(memory_space=pl.ANY)
+        hbm = pl.BlockSpec(memory_space=pltpu.HBM)
         dma = pltpu.SemaphoreType.DMA
         flops = 2 * row_count * nb * (nb + columns)
         return pl.pallas_call(
             functools.partial(kernel, n_x, n_z, parts),
-            out_shape=jax.ShapeDtypeStruct(slab.shape, slab.dtype),
+            out_shape=pltpu.VMEM(slab.shape, slab.dtype),
             in_specs=[
-                any_space,
-                any_space,
+                hbm,
+                hbm,
                 pl.BlockSpec(memory_space=pltpu.SMEM),
                 pl.BlockSpec(memory_space=pltpu.VMEM),
-                any_space,
-                any_space,
+                hbm,
+                hbm,
             ],
-            out_specs=any_space,
+            out_specs=pl.BlockSpec(memory_space=pltpu.VMEM),
             scratch_shapes=[
-                pltpu.VMEM((row_count, columns), F32),
                 pltpu.VMEM((n_z, rows, nb), F32),
-                pltpu.VMEM((n_z, rows, nb), F32),
+                pltpu.VMEM((2, n_z, rows, nb), BF16),
                 pltpu.VMEM((n_z, rows, columns), F32),
                 pltpu.VMEM((n_z, rows, columns), F32),
                 pltpu.VMEM((nb, nb), F32),
                 pltpu.VMEM((nb, nb), F32),
+                pltpu.VMEM((2, nb, nb), BF16),
                 pltpu.VMEM((2, nb, half), F32),
                 pltpu.VMEM((nb, half), F32),
                 pltpu.VMEM((nb, half), F32),
                 pltpu.VMEM((max(n_x - 1, 1), nb, half), F32),
                 pltpu.VMEM((nb, half), F32),
                 pltpu.VMEM((4, nb, half), F32),
-                pltpu.VMEM((nb, columns), F32),
-                pltpu.VMEM((nb, columns), F32),
+                pltpu.VMEM((2, nb, 2 * columns), BF16),
                 dma((4,)),
                 dma((links,)),
                 dma((links,)),
                 dma((n_z * parts,)),
                 dma((n_z * parts,)),
-                dma((2 * n_z * parts,)),
                 dma,
                 dma,
                 dma((max(n_x - 1, 1),)),
@@ -365,12 +381,17 @@
                 dma((3,)),
             ],
             compiler_params=pltpu.CompilerParams(
-                collective_id=0, has_side_effects=True, vmem_limit_bytes=60 * 2**20
+                collective_id=0, has_side_effects=True, vmem_limit_bytes=32 * 2**20
             ),
             cost_estimate=pl.CostEstimate(
                 flops=flops, bytes_accessed=8 * slab.size, transcendentals=0
             ),
-        )(slab, panel, pivots, pivots.reshape(1, nb), inv_lower, inv_upper)
+        )(
+            *(pltpu.with_memory_space_constraint(a, pltpu.HBM) for a in (slab, panel)),
+            pivots,
+            pivots.reshape(1, nb),
+            *(pltpu.with_memory_space_constraint(a, pltpu.HBM) for a in (inv_lower, inv_upper)),
+        )
 
     return jax.shard_map(
         local,

time: 86.3 us -> 83.4 us (0.966)
  local copies, waits for them, and re-layouts: 4.47 us -> 2.7 us
  Pallas kernels: 81.7 us -> 80.6 us
    unnamed x1 -> x3, local copies, waits for them, and re-layouts: 4.47 us -> 2.7 us
    pallas_call x1, Pallas kernels: 81.7 us -> 80.6 us  [local(): pl.pallas_call(functools.partial(kernel, n_x, n_z, parts), out_shape=pltp...]
where the time goes in v2:
time: 83.4 us; the launch traced here: 83.3 us
  Pallas kernels  80.6 us (97%)
  local copies, waits for them, and re-layouts  2.7 us (3%)
    pallas_call x1, Pallas kernels, local(): pl.pallas_call(functools.partial(kernel, n_x, n_z, parts), out_shape=pltp...  80.6 us
    unnamed x3, local copies, waits for them, and re-layouts  2.7 us

profile of v2, /device:TPU:0, one launch (start us, length us, event | category | flops | bytes accessed | tf_op | source)
XLA Modules:
  0.0 83.3 jit_solution(3166768678619464550)
XLA Ops:
  0.0 0.0 copy-start
  0.0 0.7 copy-done
  0.7 80.6 %shard_map.55 = f32[4096,256]{1,0:T(8,128)S(1)} custom-call(f32[4096,256]{1,0:T(8,128)} %slab_ref.1, f32[512,512]{1,0:T(8,128)} %panel_ref.1, s32[512]{0:T(512)S(1)} %copy-done, s32[1,512]{1,0:T(1,128)S(1)} %bitcast.1, f32[512,512]{1,0:T(8,128)} %inv_lower_ref.1, f32[512,512]{1,0:T(8,128)} %inv_upper_ref.1), custom_call_target="tpu_custom_call" | custom-call | flops 3221225472 | bytes 8388608 | tf_op jit(solution)/shard_map/pallas_call | solution.py:344
  81.3 2.0 %copy.7 = f32[4096,256]{1,0:T(8,128)} copy(f32[4096,256]{1,0:T(8,128)S(1)} %shard_map.55) | data formatting | bytes 8388608
Async XLA Ops:
  0.0 0.7 copy-start

commit v3 on v2

--- a/solution.py
+++ b/solution.py
@@ -38,7 +38,7 @@
     raw, lower, stage, landed, inv_lower, inv_upper, inv_split,
     picked, partner_part, chip_sum, from_x, total, halves, upper,
     load_sem, link_send, link_recv, product_send, product_recv,
-    pick_send, pick_recv, x_send, x_recv, half_send, half_recv,
+    pick_send, pick_recv, x_send, x_recv, half_send, half_recv, raw_peer, peer_send, peer_recv,
 ):
     slab = out_ref
     prow = lax.axis_index("prow")
@@ -124,6 +124,17 @@
             def _():
                 send(direction, 0, g).start()
 
+    def peer_copy(g):
+        span = pl.ds(g * piece, piece)
+        return pltpu.make_async_remote_copy(
+            src_ref=panel_ref.at[span], dst_ref=raw_peer.at[span],
+            send_sem=peer_send.at[g], recv_sem=peer_recv.at[g],
+            device_id=peer, device_id_type=MESH,
+        )
+
+    for g in range(parts):
+        peer_copy(g).start()
+
     loads[0].wait()
 
     def pick(k, carry):
@@ -264,7 +275,23 @@
         span = pl.ds(g * piece, piece)
         finish(block, 1 - y, g, landed[block, span, :], is_pivot)
 
-    lax.fori_loop(0, parts, lambda g, c: (multiply(z, g), c)[1], 0)
+    def multiply_own(g):
+        span = pl.ds(g * piece, piece)
+        _, is_pivot = pivot_hits(z, y, g)
+        product = dot_split(
+            lower[0, z, span, :], lower[1, z, span, :],
+            upper[0, :, :columns], upper[1, :, :columns],
+        )
+        finish(z, y, g, product, is_pivot)
+
+    def take_peer(g):
+        peer_copy(g).wait_recv()
+        high, low = split(raw_peer[pl.ds(g * piece, piece), :])
+        solved = dot_split(high, low, inv_split[0], inv_split[1])
+        hits, is_pivot = pivot_hits(z, 1 - y, g)
+        high, low = split(jnp.where(is_pivot, -hits, solved))
+        product = dot_split(high, low, upper[0, :, :columns], upper[1, :, :columns])
+        finish(z, 1 - y, g, product, is_pivot)
 
     def second_stage(g, carry):
         for exists, block in blocks_of(1):
@@ -274,6 +301,7 @@
         return carry
 
     lax.fori_loop(0, parts, second_stage, 0)
+    lax.fori_loop(0, parts, lambda g, c: (multiply_own(g), c)[1], 0)
 
     def late_stage(i, carry):
         stage_index, g = 2 + i // parts, i % parts
@@ -286,7 +314,7 @@
 
         @pl.when(stage_index == 2)
         def _():
-            take(z, g)
+            take_peer(g)
 
         for exists, block in blocks_of(stage_index - 2):
             @pl.when(exists & (stage_index > 2))
@@ -302,7 +330,7 @@
         if n_z == 2:
             @pl.when(stage_index == 0)
             def _():
-                take(z, g)
+                take_peer(g)
 
         for exists, block in blocks_of(stage_index):
             @pl.when(exists & (stage_index > 0))
@@ -314,7 +342,14 @@
 
     def settle(i, carry):
         block, g = i // parts, i % parts
-        product_copy(block, g).wait_send()
+
+        @pl.when(block != z)
+        def _():
+            product_copy(block, g).wait_send()
+
+        @pl.when(block == z)
+        def _():
+            peer_copy(g).wait_send()
         return carry
 
     lax.fori_loop(0, n_z * parts, settle, 0)
@@ -379,6 +414,9 @@
                 dma((max(n_x - 1, 1),)),
                 dma((3,)),
                 dma((3,)),
+                pltpu.VMEM((rows, nb), F32),
+                dma((parts,)),
+                dma((parts,)),
             ],
             compiler_params=pltpu.CompilerParams(
                 collective_id=0, has_side_effects=True, vmem_limit_bytes=32 * 2**20

time: 83.4 us -> 82.8 us (level)
  no operation moved by 1% of the time
where the time goes in v3:
time: 82.8 us; the launch traced here: 82.6 us
  Pallas kernels  79.9 us (96%)
  local copies, waits for them, and re-layouts  2.7 us (3%)
    pallas_call x1, Pallas kernels, local(): pl.pallas_call(functools.partial(kernel, n_x, n_z, parts), out_shape=pltp...  79.9 us
    unnamed x3, local copies, waits for them, and re-layouts  2.7 us

profile of v3, /device:TPU:0, one launch (start us, length us, event | category | flops | bytes accessed | tf_op | source)
XLA Modules:
  0.0 82.6 jit_solution(14424780328956516097)
XLA Ops:
  0.0 0.0 copy-start
  0.0 0.7 copy-done
  0.7 79.9 %shard_map.55 = f32[4096,256]{1,0:T(8,128)S(1)} custom-call(f32[4096,256]{1,0:T(8,128)} %slab_ref.1, f32[512,512]{1,0:T(8,128)} %panel_ref.1, s32[512]{0:T(512)S(1)} %copy-done, s32[1,512]{1,0:T(1,128)S(1)} %bitcast.1, f32[512,512]{1,0:T(8,128)} %inv_lower_ref.1, f32[512,512]{1,0:T(8,128)} %inv_upper_ref.1), custom_call_target="tpu_custom_call" | custom-call | flops 3221225472 | bytes 8388608 | tf_op jit(solution)/shard_map/pallas_call | solution.py:379
  80.6 2.0 %copy.7 = f32[4096,256]{1,0:T(8,128)} copy(f32[4096,256]{1,0:T(8,128)S(1)} %shard_map.55) | data formatting | bytes 8388608
Async XLA Ops:
  0.0 0.7 copy-start
